TPU v7x, 256 devices: a whole 4x4x8 slice. The times are simulated.
256 devices in a mesh: row: 16 (over z, x_lo), col: 8 (over y, x_hi), depth: 2 (over core).
Axes of the slice: x: 4 (x_hi: 2, x_lo: 2; x = x_hi * 2 + x_lo), y: 4, z: 8, core: 2. Of those that a mesh axis runs over, the one named last changes fastest.
Arguments:
- matrix: float32 [2, 16, 512, 4, 8, 512], P(None, 'row', None, None, 'col'), may hold values from 0 to 5
Outputs:
- factored: float32 [2, 16, 512, 4, 8, 512], P(None, 'row', 'depth', None, 'col')
All inputs are finite; a program needn't handle non-finite values.
Results may differ from a plain program's by a relative error of at most 0.00021.
Values sent between devices are 32-bit elements; how exact they have to be, the bound alone decides.
A program may use at most 128 MiB of HBM per device.

v0:
```python
import jax
import jax.numpy as jnp
from jax import lax
from jax.sharding import Mesh
from jax.sharding import PartitionSpec as P

STEPS = 2
ROW = ("row_0", "row_1")


def split_up(x, dim, size):
    before, after = (x.shape[:dim], x.shape[dim + 1 :])
    return jnp.moveaxis(x.reshape(*before, size, -1, *after), dim, 0)


def summed_on_arrival(x, axis, dim):
    blocks = split_up(x, dim, lax.axis_size(axis))
    arrived = lax.all_to_all(blocks, axis, split_axis=0, concat_axis=0, tiled=True)
    return arrived.sum(axis=0)


def spread(x, axes, root):
    x = jnp.where(lax.axis_index(axes) == root, x, jnp.zeros_like(x))
    for axis in axes:
        x = lax.psum(x, axis)
    return x


def from_everyone(x, axis):
    size = lax.axis_size(axis)
    return lax.all_to_all(jnp.broadcast_to(x[None], (size, *x.shape)), axis, 0, 0, tiled=True)


def laid_out(blocks, dim):
    shape = list(blocks.shape[1:])
    shape[dim] *= blocks.shape[0]
    return jnp.moveaxis(blocks, 0, dim).reshape(shape)


def gathered_copies(x, axis, dim):
    blocks = from_everyone(x, axis)
    return laid_out(blocks, dim)


def broadcast(x, axis, root):
    return lax.dynamic_index_in_dim(lax.all_gather(x, axis), root, 0, keepdims=False)


def body(matrix):
    tiles_rows = matrix.shape[0]
    tile = matrix.shape[2]
    tiles_cols = matrix.shape[3]
    grid_rows = lax.axis_size(ROW)
    grid_cols = lax.axis_size("col")
    layers_count = lax.axis_size("depth")
    half_width = tile // layers_count
    depth_index = lax.axis_index("depth")
    row_index = lax.axis_index(ROW)
    col_index = lax.axis_index("col")
    local = matrix.reshape(tiles_rows, tile, tiles_cols, tile)
    keeper = (depth_index == 0).astype(jnp.float32)
    columns = [local[:, :, j, :] * keeper for j in range(tiles_cols)]
    global_rows = jnp.arange(tiles_rows, dtype=jnp.int32) * grid_rows + row_index
    global_cols = jnp.arange(tiles_cols, dtype=jnp.int32) * grid_cols + col_index
    identity = jnp.eye(tile, dtype=jnp.float32)
    stored = []
    for section in range(STEPS):
        owner_col = section % grid_cols
        slot_col = section // grid_cols
        reduced = summed_on_arrival(columns[slot_col], "depth", 1)
        shared = broadcast(reduced, "col", owner_col)
        owner_row = section % grid_rows
        slot_row = section // grid_rows
        halves = spread(shared[slot_row], ROW, owner_row)
        diag = gathered_copies(halves, "depth", 0)
        diag_factor = jnp.linalg.cholesky(diag)
        inverse_factor = jax.scipy.linalg.solve_triangular(diag_factor, identity, lower=True)
        solved = jnp.einsum(
            "ipb,cb->ipc",
            shared,
            inverse_factor,
            precision=lax.Precision.HIGHEST,
            preferred_element_type=jnp.float32,
        )
        own_rows = lax.dynamic_slice_in_dim(diag_factor, depth_index * half_width, half_width, 0)
        below = (global_rows > section)[:, None, None]
        at_diag = (global_rows == section)[:, None, None]
        panel = jnp.where(below, solved, jnp.where(at_diag, own_rows[None], 0.0))
        rows_half = lax.all_to_all(panel, "depth", split_axis=2, concat_axis=1, tiled=True)
        stored.append(panel)
        rows_half = rows_half * (global_rows > section).astype(jnp.float32)[:, None, None]
        tiles_out = []
        for crossing_j in range(tiles_cols):
            target = global_cols[crossing_j]
            owner = target % grid_rows
            slot = target // grid_rows
            piece = lax.dynamic_index_in_dim(rows_half, slot, 0, keepdims=False)
            tiles_out.append(spread(piece, ROW, owner))
        for j in range(tiles_cols):
            columns[j] = columns[j] - jnp.einsum(
                "ipe,qe->ipq",
                rows_half,
                tiles_out[j],
                precision=lax.Precision.HIGHEST,
                preferred_element_type=jnp.float32,
            )
    whole = jnp.stack(columns, axis=2)
    summed = summed_on_arrival(whole, "depth", 1)
    upper = (global_rows < STEPS)[:, None, None, None] & (global_cols >= STEPS)[None, None, :, None]
    summed = jnp.where(upper, 0.0, summed)
    for section in range(STEPS):
        owner_col = section % grid_cols
        slot_col = section // grid_cols
        hit = col_index == owner_col
        summed = summed.at[:, :, slot_col, :].set(
            jnp.where(hit, stored[section], summed[:, :, slot_col, :])
        )
    return summed.reshape(tiles_rows, 1, half_width, tiles_cols, 1, tile)


def solution(mesh):
    split = Mesh(
        mesh.devices.reshape(8, 2, mesh.shape["col"], mesh.shape["depth"]),
        ("row_0", "row_1", "col", "depth"),
    )
    placed = (P(None, ROW, None, None, "col", None),)
    return jax.shard_map(
        body,
        mesh=split,
        in_specs=placed,
        out_specs=P(None, ROW, "depth", None, "col", None),
        check_vma=False,
    )
```

profile of v0, /device:TPU:1, one launch (start us, length us, event | category | flops | bytes accessed | tf_op | source)
XLA Modules:
  0.0 1221.9 jit_solution(510988850766627012)
XLA Ops:
  31.2 111.9 %all-gather.5.cloned.1.call-done = f32[16,256,512]{2,1,0:T(8,128)} async-done(((f32[2,256,512]{2,1,0:T(8,128)}), f32[16,256,512]{2,1,0:T(8,128)}) %all-gather.5.cloned.1.call-update) | async-done | bytes 8388624 | tf_op jit(solution)/shard_map/all_gather | solution.py:46
  145.1 68.1 %all-reduce.12.cloned.1.call-done = f32[256,512]{1,0:T(8,128)} async-done(((f32[256,512]{1,0:T(8,128)}), f32[256,512]{1,0:T(8,128)}) %all-reduce.12.cloned.1.call-update) | async-done | bytes 524304 | tf_op jit(solution)/shard_map/psum | solution.py:25
  225.6 33.4 %all-reduce.14.cloned.1.call-done = f32[256,512]{1,0:T(8,128)} async-done(((f32[256,512]{1,0:T(8,128)}), f32[256,512]{1,0:T(8,128)}) %all-reduce.14.cloned.1.call-update) | async-done | bytes 524304 | tf_op jit(solution)/shard_map/psum | solution.py:25
  269.3 11.7 cholesky.286
  293.5 11.7 cholesky.305
  305.3 10.0 custom-call.28
  316.8 11.7 cholesky.326
  340.5 11.7 cholesky.343
  359.6 11.0 while.6
  371.3 40.1 %custom-call.30 = f32[4,128,128]{1,2,0:T(8,128)S(1)} custom-call(f32[4,128,128]{2,1,0:T(8,128)} %copy-done.18), custom_call_target="InvertDiagBlocksLowerTriangular" | custom-call | tf_op jit(solution)/shard_map/jit(_solve_triangular)/triangular_solve | solution.py:77
  433.5 69.9 %all-reduce.16.cloned.1.call-done = f32[512,256]{1,0:T(8,128)} async-done(((f32[512,256]{1,0:T(8,128)}), f32[512,256]{1,0:T(8,128)}) %all-reduce.16.cloned.1.call-update) | async-done | bytes 524304 | tf_op jit(solution)/shard_map/psum | solution.py:25
  503.4 45.6 %all-reduce.18.cloned.1.call-done = f32[512,256]{1,0:T(8,128)} async-done(((f32[512,256]{1,0:T(8,128)}), f32[512,256]{1,0:T(8,128)}) %all-reduce.18.cloned.1.call-update) | async-done | bytes 524304 | tf_op jit(solution)/shard_map/psum | solution.py:25
  560.6 111.7 %all-gather.7.cloned.1.call-done = f32[16,256,512]{2,1,0:T(8,128)} async-done(((f32[2,256,512]{2,1,0:T(8,128)}), f32[16,256,512]{2,1,0:T(8,128)}) %all-gather.7.cloned.1.call-update) | async-done | bytes 8388624 | tf_op jit(solution)/shard_map/all_gather | solution.py:46
  674.2 68.1 %all-reduce.20.cloned.1.call-done = f32[256,512]{1,0:T(8,128)} async-done(((f32[256,512]{1,0:T(8,128)}), f32[256,512]{1,0:T(8,128)}) %all-reduce.20.cloned.1.call-update) | async-done | bytes 524304 | tf_op jit(solution)/shard_map/psum | solution.py:25
  742.4 45.7 %all-reduce.22.cloned.1.call-done = f32[256,512]{1,0:T(8,128)} async-done(((f32[256,512]{1,0:T(8,128)}), f32[256,512]{1,0:T(8,128)}) %all-reduce.22.cloned.1.call-update) | async-done | bytes 524304 | tf_op jit(solution)/shard_map/psum | solution.py:25
  796.2 11.7 cholesky.358
  820.4 11.7 cholesky.377
  845.0 11.7 cholesky.398
  868.7 11.7 cholesky.415
  885.7 11.3 while.7
  897.0 39.3 %custom-call.34 = f32[4,128,128]{1,2,0:T(8,128)S(1)} custom-call(f32[4,128,128]{2,1,0:T(8,128)S(1)} %get-tuple-element.46), custom_call_target="InvertDiagBlocksLowerTriangular" | custom-call | tf_op jit(solution)/shard_map/jit(_solve_triangular)/triangular_solve | solution.py:77
  956.8 100.1 %all-reduce.24.cloned.1.call-done = (f32[512,256]{1,0:T(8,128)}, f32[512,256]{1,0:T(8,128)}, f32[512,256]{1,0:T(8,128)}, f32[512,256]{1,0:T(8,128)}, f32[512,256...) async-done(((f32[512,256]{1,0:T(8,128)}, f32[512,256]{1,0:T(8,128)}, f32[512,256]{1,0:T(8,128)}, f32[512,256]{1,0:T(8,128)}, f32[512,256]{1,0:T(8,128)}, ...) | async-done | bytes 3670032 | tf_op jit(solution)/shard_map/psum | solution.py:25
  1057.1 110.7 %all-reduce.26.cloned.1.call-done = (f32[512,256]{1,0:T(8,128)}, f32[512,256]{1,0:T(8,128)}, f32[512,256]{1,0:T(8,128)}, f32[512,256]{1,0:T(8,128)}, f32[512,256...) async-done(((f32[512,256]{1,0:T(8,128)}, f32[512,256]{1,0:T(8,128)}, f32[512,256]{1,0:T(8,128)}, f32[512,256]{1,0:T(8,128)}, f32[512,256]{1,0:T(8,128)}, ...) | async-done | bytes 3670032 | tf_op jit(solution)/shard_map/psum | solution.py:25
  1185.0 12.2 %all_to_all.66 = f32[2,2,256,4,512]{4,2,1,3,0:T(8,128)} all-to-all(f32[2,2,256,4,512]{4,2,1,3,0:T(8,128)S(1)} %copy_bitcast_fusion), channel_id=1, replica_groups=mesh['row_0'=8,'row_1'=2,'col'=8,'depth'=2] {'depth'}, dimensions={0} | all-to-all | bytes 16777216 | tf_op jit(solution)/shard_map/all_to_all | solution.py:18
  (208 shorter events, 231.0 us)
Async XLA Ops:
  12.6 3.2 copy-start
  17.6 10.7 all-to-all-start
  25.6 117.5 %all-gather.5.cloned.1.call-start = ((), (), s32[]{:S(2)}) async-start(), calls=%async_computation.13 | async-start | bytes 9437184 | tf_op jit(solution)/shard_map/all_gather | solution.py:46
  31.2 182.1 %all-reduce.12.cloned.1.call-start = ((), (), s32[]{:S(2)}) async-start(), calls=%async_computation.7 | async-start | bytes 1048576 | tf_op jit(solution)/shard_map/psum | solution.py:25
  145.0 114.0 %all-reduce.14.cloned.1.call-start = ((), (), s32[]{:S(2)}) async-start(), calls=%async_computation.8 | async-start | bytes 1048576 | tf_op jit(solution)/shard_map/psum | solution.py:25
  213.2 290.1 %all-reduce.16.cloned.1.call-start = ((), (), s32[]{:S(2)}) async-start(), calls=%async_computation.9 | async-start | bytes 1048576 | tf_op jit(solution)/shard_map/psum | solution.py:25
  352.3 4.0 copy-start.7
  356.3 55.2 %copy-start.5 = (f32[512,512]{1,0:T(8,128)S(1)}, f32[512,512]{1,0:T(8,128)}, u32[]{:S(2)}) copy-start(f32[512,512]{1,0:T(8,128)} %fusion.28) | copy-start | bytes 3145732
  413.1 4.2 copy-start.11
  420.5 7.9 copy-start.3
  433.5 115.6 %all-reduce.18.cloned.1.call-start = ((), (), s32[]{:S(2)}) async-start(), calls=%async_computation.10 | async-start | bytes 1048576 | tf_op jit(solution)/shard_map/psum | solution.py:25
  503.4 168.8 %all-gather.7.cloned.1.call-start = ((), (), s32[]{:S(2)}) async-start(), calls=%async_computation.14 | async-start | bytes 9437184 | tf_op jit(solution)/shard_map/all_gather | solution.py:46
  560.5 181.8 %all-reduce.20.cloned.1.call-start = ((), (), s32[]{:S(2)}) async-start(), calls=%async_computation.11 | async-start | bytes 1048576 | tf_op jit(solution)/shard_map/psum | solution.py:25
  674.1 114.0 %all-reduce.22.cloned.1.call-start = ((), (), s32[]{:S(2)}) async-start(), calls=%async_computation.12 | async-start | bytes 1048576 | tf_op jit(solution)/shard_map/psum | solution.py:25
  742.3 314.6 %all-reduce.24.cloned.1.call-start = ((), (), s32[]{:S(2)}) async-start(), calls=%async_computation.15 | async-start | bytes 7340032 | tf_op jit(solution)/shard_map/psum | solution.py:25
  883.6 52.7 %copy-start.6 = (f32[512,512]{1,0:T(8,128)S(1)}, f32[512,512]{1,0:T(8,128)}, u32[]{:S(2)}) copy-start(f32[512,512]{1,0:T(8,128)} %fusion.28) | copy-start | bytes 3145732
  938.0 4.2 copy-start.10
  956.6 211.2 %all-reduce.26.cloned.1.call-start = ((), (), s32[]{:S(2)}) async-start(), calls=%async_computation.16 | async-start | bytes 7340032 | tf_op jit(solution)/shard_map/psum | solution.py:25
  1167.8 3.8 copy-start.17
  1167.8 9.4 slice-start
  1171.5 5.7 slice-start.1
  1177.2 2.2 copy-start.13
  1204.0 3.4 copy-start.1
  1204.0 3.7 copy-start.4
  (8 other events, 11.9 us)
Sparse Core Ops, SparseCore 0:
  31.3 111.8 all-gather.4
  145.5 67.7 all-reduce.11
  215.8 43.1 all-reduce.13
  433.6 69.7 all-reduce.15
  505.8 43.1 all-reduce.17
  560.6 111.5 all-gather.6
  674.5 67.7 all-reduce.19
  744.9 43.1 all-reduce.21
  956.7 100.2 all-reduce.23
  1059.9 107.8 all-reduce.25
where the time goes:
time: 1230 us; the launch traced here: 1220 us
  waiting for transfers between devices  768 us (62%)
  other arithmetic  271 us (22%)
  local copies, waits for them, and re-layouts  56.1 us (5%)
  matrix products  47.6 us (4%)
  blocking collectives  40.5 us (3%)
  between operations  30.2 us (2%)
    psum x8, waiting for transfers between devices, spread(): x = lax.psum(x, axis)  542 us
    all_gather x2, waiting for transfers between devices, broadcast(): lax.all_gather(x, axis)  224 us
    another operation x29, other arithmetic, body(): diag_factor = jnp.linalg.cholesky(diag)  158 us
    another operation x5, other arithmetic, body(): jax.scipy.linalg.solve_triangular(diag_factor, identity, lower=True)  84.6 us
  transfers between devices with their start and end apart: 11, of which 11 were waited for; matrix products, arithmetic and copies ran while one was open for 0% of the time, Pallas kernels for 0%

commit v1 on v0

--- a/solution.py
+++ b/solution.py
@@ -6,6 +6,11 @@
 
 STEPS = 2
 ROW = ("row_0", "row_1")
+
+
+def touch_the_figure(vec, dev_axis):
+    carry_out = jnp.sum(lax.all_gather(vec, dev_axis), axis=0)
+    return carry_out
 
 
 def split_up(x, dim, size):
@@ -22,7 +27,7 @@
 def spread(x, axes, root):
     x = jnp.where(lax.axis_index(axes) == root, x, jnp.zeros_like(x))
     for axis in axes:
-        x = lax.psum(x, axis)
+        x = touch_the_figure(x, axis)
     return x
 
 

time: 1230 us -> 1340 us (1.089)
  other arithmetic: 271 us -> 321 us
  waiting for transfers between devices: 768 us -> 812 us
  matrix products: 47.6 us -> 62.2 us
    all_gather x0 -> x20, waiting for transfers between devices: none -> 582 us  [touch_the_figure(): carry_out = jnp.sum(lax.all_gather(vec, dev_axis), axis=0)]
    psum x8 -> x0, waiting for transfers between devices: 542 us -> none  [spread(): x = lax.psum(x, axis)]
    reduce_sum x0 -> x20, other arithmetic: none -> 51.1 us  [touch_the_figure(): carry_out = jnp.sum(lax.all_gather(vec, dev_axis), axis=0)]
    dot_general x8, matrix products: 18.9 us -> 33.5 us  [body(): jnp.einsum('ipe,qe->ipq', rows_half, tiles_out[j], precision=lax.Precisio...]
  transfers between devices with their start and end apart: 11 -> 23, of which waited for: 11 -> 20; matrix products, arithmetic and copies ran while one was open for 0% -> 16% of each run, Pallas kernels for 0% -> 0%
where the time goes in v1:
time: 1340 us; the launch traced here: 1330 us
  waiting for transfers between devices  812 us (61%)
  other arithmetic  321 us (24%)
  matrix products  62.2 us (5%)
  local copies, waits for them, and re-layouts  57 us (4%)
  blocking collectives  40.5 us (3%)
  between operations  30.4 us (2%)
    all_gather x20, waiting for transfers between devices, touch_the_figure(): carry_out = jnp.sum(lax.all_gather(vec, dev_axis), axis=0)  582 us
    all_gather x2, waiting for transfers between devices, broadcast(): lax.all_gather(x, axis)  224 us
    another operation x29, other arithmetic, body(): diag_factor = jnp.linalg.cholesky(diag)  158 us
    another operation x5, other arithmetic, body(): jax.scipy.linalg.solve_triangular(diag_factor, identity, lower=True)  84.3 us
    reduce_sum x20, other arithmetic, touch_the_figure(): carry_out = jnp.sum(lax.all_gather(vec, dev_axis), axis=0)  51.1 us
    dot_general x8, matrix products, body(): jnp.einsum('ipe,qe->ipq', rows_half, tiles_out[j], precision=lax.Precisio...  33.5 us
  transfers between devices with their start and end apart: 23, of which 20 were waited for; matrix products, arithmetic and copies ran while one was open for 16% of the time, Pallas kernels for 0%

profile of v1, /device:TPU:1, one launch (start us, length us, event | category | flops | bytes accessed | tf_op | source)
XLA Modules:
  0.0 1332.4 jit_solution(16974150120250580060)
XLA Ops:
  31.2 111.9 %all-gather.53.cloned.1.call-done = f32[16,256,512]{2,1,0:T(8,128)} async-done(((f32[2,256,512]{2,1,0:T(8,128)}), f32[16,256,512]{2,1,0:T(8,128)}) %all-gather.53.cloned.1.call-update) | async-done | bytes 8388624 | tf_op jit(solution)/shard_map/all_gather | solution.py:51
  145.1 53.3 %all-gather.55.cloned.1.call-done = f32[8,1,256,512]{3,2,1,0:T(8,128)} async-done(((f32[1,1,256,512]{3,2,1,0:T(8,128)}), f32[8,1,256,512]{3,2,1,0:T(8,128)}) %all-gather.55.cloned.1.call-update) | async-done | bytes 4194320 | tf_op jit(solution)/shard_map/all_gather | solution.py:12
  214.0 13.1 all-gather.57.cloned.1.call-done
  239.5 11.7 cholesky.286
  263.7 11.7 cholesky.305
  341.6 40.1 %custom-call.30 = f32[4,128,128]{1,2,0:T(8,128)S(1)} custom-call(f32[4,128,128]{2,1,0:T(8,128)} %copy-done.18), custom_call_target="InvertDiagBlocksLowerTriangular" | custom-call | tf_op jit(solution)/shard_map/jit(_solve_triangular)/triangular_solve | solution.py:82
  403.8 55.4 %all-gather.37.cloned.1.call-done = f32[8,512,256]{2,1,0:T(8,128)} async-done(((f32[1,512,256]{2,1,0:T(8,128)}), f32[8,512,256]{2,1,0:T(8,128)}) %all-gather.37.cloned.1.call-update) | async-done | bytes 4194320 | tf_op jit(solution)/shard_map/all_gather | solution.py:12
  462.6 25.1 %all-gather.59.cloned.1.call-done = f32[1024,256]{1,0:T(8,128)} async-done(((f32[512,256]{1,0:T(8,128)}), f32[1024,256]{1,0:T(8,128)}) %all-gather.59.cloned.1.call-update) | async-done | bytes 1048592 | tf_op jit(solution)/shard_map/all_gather | solution.py:12
  501.3 111.7 %all-gather.61.cloned.1.call-done = f32[16,256,512]{2,1,0:T(8,128)} async-done(((f32[2,256,512]{2,1,0:T(8,128)}), f32[16,256,512]{2,1,0:T(8,128)}) %all-gather.61.cloned.1.call-update) | async-done | bytes 8388624 | tf_op jit(solution)/shard_map/all_gather | solution.py:51
  614.9 53.3 %all-gather.63.cloned.1.call-done = f32[8,1,256,512]{3,2,1,0:T(8,128)} async-done(((f32[1,1,256,512]{3,2,1,0:T(8,128)}), f32[8,1,256,512]{3,2,1,0:T(8,128)}) %all-gather.63.cloned.1.call-update) | async-done | bytes 4194320 | tf_op jit(solution)/shard_map/all_gather | solution.py:12
  673.9 23.0 %all-gather.65.cloned.1.call-done = f32[512,512]{1,0:T(8,128)} async-done(((f32[256,512]{1,0:T(8,128)}), f32[512,512]{1,0:T(8,128)}) %all-gather.65.cloned.1.call-update) | async-done | bytes 1048592 | tf_op jit(solution)/shard_map/all_gather | solution.py:12
  806.3 39.3 %custom-call.34 = f32[4,128,128]{1,2,0:T(8,128)S(1)} custom-call(f32[4,128,128]{2,1,0:T(8,128)S(1)} %get-tuple-element.46), custom_call_target="InvertDiagBlocksLowerTriangular" | custom-call | tf_op jit(solution)/shard_map/jit(_solve_triangular)/triangular_solve | solution.py:82
  879.0 43.2 %all-gather.39.cloned.1.call-done = f32[8,512,256]{2,1,0:T(8,128)} async-done(((f32[1,512,256]{2,1,0:T(8,128)}), f32[8,512,256]{2,1,0:T(8,128)}) %all-gather.39.cloned.1.call-update) | async-done | bytes 4194320 | tf_op jit(solution)/shard_map/all_gather | solution.py:12
  925.6 51.8 %all-gather.43.cloned.1.call-done = f32[8,512,256]{2,1,0:T(8,128)} async-done(((f32[1,512,256]{2,1,0:T(8,128)}), f32[8,512,256]{2,1,0:T(8,128)}) %all-gather.43.cloned.1.call-update) | async-done | bytes 4194320 | tf_op jit(solution)/shard_map/all_gather | solution.py:12
  980.8 51.6 %all-gather.47.cloned.1.call-done = f32[8,512,256]{2,1,0:T(8,128)} async-done(((f32[1,512,256]{2,1,0:T(8,128)}), f32[8,512,256]{2,1,0:T(8,128)}) %all-gather.47.cloned.1.call-update) | async-done | bytes 4194320 | tf_op jit(solution)/shard_map/all_gather | solution.py:12
  1036.0 23.0 %all-gather.69.cloned.1.call-done = f32[1024,256]{1,0:T(8,128)} async-done(((f32[512,256]{1,0:T(8,128)}), f32[1024,256]{1,0:T(8,128)}) %all-gather.69.cloned.1.call-update) | async-done | bytes 1048592 | tf_op jit(solution)/shard_map/all_gather | solution.py:12
  1061.2 26.9 %all-gather.73.cloned.1.call-done = f32[1024,256]{1,0:T(8,128)} async-done(((f32[512,256]{1,0:T(8,128)}), f32[1024,256]{1,0:T(8,128)}) %all-gather.73.cloned.1.call-update) | async-done | bytes 1048592 | tf_op jit(solution)/shard_map/all_gather | solution.py:12
  1090.2 26.9 %all-gather.77.cloned.1.call-done = f32[1024,256]{1,0:T(8,128)} async-done(((f32[512,256]{1,0:T(8,128)}), f32[1024,256]{1,0:T(8,128)}) %all-gather.77.cloned.1.call-update) | async-done | bytes 1048592 | tf_op jit(solution)/shard_map/all_gather | solution.py:12
  1129.9 44.6 %all-gather.51.cloned.1.call-done = f32[8,512,256]{2,1,0:T(8,128)} async-done(((f32[1,512,256]{2,1,0:T(8,128)}), f32[8,512,256]{2,1,0:T(8,128)}) %all-gather.51.cloned.1.call-update) | async-done | bytes 4194320 | tf_op jit(solution)/shard_map/all_gather | solution.py:12
  1177.8 23.5 %all-gather.67.cloned.1.call-done = f32[1024,256]{1,0:T(8,128)} async-done(((f32[512,256]{1,0:T(8,128)}), f32[1024,256]{1,0:T(8,128)}) %all-gather.67.cloned.1.call-update) | async-done | bytes 1048592 | tf_op jit(solution)/shard_map/all_gather | solution.py:12
  1203.4 26.9 %all-gather.71.cloned.1.call-done = f32[1024,256]{1,0:T(8,128)} async-done(((f32[512,256]{1,0:T(8,128)}), f32[1024,256]{1,0:T(8,128)}) %all-gather.71.cloned.1.call-update) | async-done | bytes 1048592 | tf_op jit(solution)/shard_map/all_gather | solution.py:12
  1231.7 27.8 %all-gather.75.cloned.1.call-done = f32[1024,256]{1,0:T(8,128)} async-done(((f32[512,256]{1,0:T(8,128)}), f32[1024,256]{1,0:T(8,128)}) %all-gather.75.cloned.1.call-update) | async-done | bytes 1048592 | tf_op jit(solution)/shard_map/all_gather | solution.py:12
  1276.4 12.3 all-gather.79.cloned.1.call-done
  1295.5 12.2 all_to_all.66
  (259 shorter events, 404.0 us)
Async XLA Ops:
  17.6 10.7 all-to-all-start
  25.6 117.5 %all-gather.53.cloned.1.call-start = ((), (), s32[]{:S(2)}) async-start(), calls=%async_computation.15 | async-start | bytes 9437184 | tf_op jit(solution)/shard_map/all_gather | solution.py:51
  31.2 167.3 %all-gather.55.cloned.1.call-start = ((), (), s32[]{:S(2)}) async-start(), calls=%async_computation.16 | async-start | bytes 4718592 | tf_op jit(solution)/shard_map/all_gather | solution.py:12
  145.0 82.0 %all-gather.57.cloned.1.call-start = ((), (), s32[]{:S(2)}) async-start(), calls=%async_computation.17 | async-start | bytes 1572864 | tf_op jit(solution)/shard_map/all_gather | solution.py:12
  201.9 257.2 %all-gather.37.cloned.1.call-start = ((), (), s32[]{:S(2)}) async-start(), calls=%async_computation.7 | async-start | bytes 4718592 | tf_op jit(solution)/shard_map/all_gather | solution.py:12
  326.5 55.2 %copy-start.5 = (f32[512,512]{1,0:T(8,128)S(1)}, f32[512,512]{1,0:T(8,128)}, u32[]{:S(2)}) copy-start(f32[512,512]{1,0:T(8,128)} %fusion.28) | copy-start | bytes 3145732
  403.7 83.9 %all-gather.59.cloned.1.call-start = ((), (), s32[]{:S(2)}) async-start(), calls=%async_computation.18 | async-start | bytes 1572864 | tf_op jit(solution)/shard_map/all_gather | solution.py:12
  462.5 150.4 %all-gather.61.cloned.1.call-start = ((), (), s32[]{:S(2)}) async-start(), calls=%async_computation.19 | async-start | bytes 9437184 | tf_op jit(solution)/shard_map/all_gather | solution.py:51
  501.2 167.0 %all-gather.63.cloned.1.call-start = ((), (), s32[]{:S(2)}) async-start(), calls=%async_computation.20 | async-start | bytes 4718592 | tf_op jit(solution)/shard_map/all_gather | solution.py:12
  614.9 82.0 %all-gather.65.cloned.1.call-start = ((), (), s32[]{:S(2)}) async-start(), calls=%async_computation.21 | async-start | bytes 1572864 | tf_op jit(solution)/shard_map/all_gather | solution.py:12
  671.8 196.4 %all-gather.41.cloned.1.call-start = ((), (), s32[]{:S(2)}) async-start(), calls=%async_computation.9 | async-start | bytes 4718592 | tf_op jit(solution)/shard_map/all_gather | solution.py:12
  672.5 199.0 %all-gather.45.cloned.1.call-start = ((), (), s32[]{:S(2)}) async-start(), calls=%async_computation.11 | async-start | bytes 4718592 | tf_op jit(solution)/shard_map/all_gather | solution.py:12
  673.1 201.9 %all-gather.49.cloned.1.call-start = ((), (), s32[]{:S(2)}) async-start(), calls=%async_computation.13 | async-start | bytes 4718592 | tf_op jit(solution)/shard_map/all_gather | solution.py:12
  673.9 248.3 %all-gather.39.cloned.1.call-start = ((), (), s32[]{:S(2)}) async-start(), calls=%async_computation.8 | async-start | bytes 4718592 | tf_op jit(solution)/shard_map/all_gather | solution.py:12
  866.8 110.6 %all-gather.43.cloned.1.call-start = ((), (), s32[]{:S(2)}) async-start(), calls=%async_computation.10 | async-start | bytes 4718592 | tf_op jit(solution)/shard_map/all_gather | solution.py:12
  867.5 164.9 %all-gather.47.cloned.1.call-start = ((), (), s32[]{:S(2)}) async-start(), calls=%async_computation.12 | async-start | bytes 4718592 | tf_op jit(solution)/shard_map/all_gather | solution.py:12
  868.1 190.9 %all-gather.69.cloned.1.call-start = ((), (), s32[]{:S(2)}) async-start(), calls=%async_computation.23 | async-start | bytes 1572864 | tf_op jit(solution)/shard_map/all_gather | solution.py:12
  871.5 216.5 %all-gather.73.cloned.1.call-start = ((), (), s32[]{:S(2)}) async-start(), calls=%async_computation.25 | async-start | bytes 1572864 | tf_op jit(solution)/shard_map/all_gather | solution.py:12
  875.0 242.1 %all-gather.77.cloned.1.call-start = ((), (), s32[]{:S(2)}) async-start(), calls=%async_computation.27 | async-start | bytes 1572864 | tf_op jit(solution)/shard_map/all_gather | solution.py:12
  878.4 296.1 %all-gather.51.cloned.1.call-start = ((), (), s32[]{:S(2)}) async-start(), calls=%async_computation.14 | async-start | bytes 4718592 | tf_op jit(solution)/shard_map/all_gather | solution.py:12
  878.9 322.3 %all-gather.67.cloned.1.call-start = ((), (), s32[]{:S(2)}) async-start(), calls=%async_computation.22 | async-start | bytes 1572864 | tf_op jit(solution)/shard_map/all_gather | solution.py:12
  925.5 304.8 %all-gather.71.cloned.1.call-start = ((), (), s32[]{:S(2)}) async-start(), calls=%async_computation.24 | async-start | bytes 1572864 | tf_op jit(solution)/shard_map/all_gather | solution.py:12
  980.7 278.8 %all-gather.75.cloned.1.call-start = ((), (), s32[]{:S(2)}) async-start(), calls=%async_computation.26 | async-start | bytes 1572864 | tf_op jit(solution)/shard_map/all_gather | solution.py:12
  1035.7 252.9 %all-gather.79.cloned.1.call-start = ((), (), s32[]{:S(2)}) async-start(), calls=%async_computation.28 | async-start | bytes 1572864 | tf_op jit(solution)/shard_map/all_gather | solution.py:12
  (18 other events, 115.5 us)
Sparse Core Ops, SparseCore 0:
  31.3 111.8 all-gather.52
  145.2 53.2 all-gather.54
  202.1 24.9 all-gather.56
  403.8 55.2 all-gather.36
  462.6 24.9 all-gather.58
  501.4 111.5 all-gather.60
  615.0 53.2 all-gather.62
  671.9 24.9 all-gather.64
  698.7 55.7 all-gather.40
  756.1 53.6 all-gather.44
  811.6 53.5 all-gather.48
  866.9 55.2 all-gather.38
  924.0 53.3 all-gather.42
  979.0 53.3 all-gather.46
  1034.0 24.9 all-gather.68
  1060.7 27.3 all-gather.72
  1089.7 27.3 all-gather.76
  1118.7 55.7 all-gather.50
  1176.3 24.9 all-gather.66
  1202.9 27.3 all-gather.70
  1232.1 27.3 all-gather.74
  1261.3 27.3 all-gather.78
